TPU v7x, 16 devices: a 4x2x1 block of a 4x4x8 slice. The times are simulated.
16 devices in a mesh: rep: 4 (over y, z, core), dp: 4 (over x).
Axes of the slice: x: 4, y: 2, z: 1, core: 2. Of those that a mesh axis runs over, the one named last changes fastest.
The devices are a block of a 4x4x8 slice.
Arguments:
- x: bfloat16 [16, 4096, 896], P(('rep', 'dp')), parts along dimension 0
- dy: bfloat16 [16, 4096, 896], P(('rep', 'dp')), parts along dimension 0
- w_gate: bfloat16 [2, 896, 2560], P(None, 'dp')
- w_up: bfloat16 [2, 896, 2560], P(None, 'dp')
- w_down: bfloat16 [2, 2560, 896], P(None, 'dp')
Outputs:
- output 1: bfloat16 [16, 4096, 896], P(('rep', 'dp')), parts along dimension 0
- output 2: bfloat16 [8, 896, 2560], P('rep', 'dp'), parts along dimension 0
- output 3: bfloat16 [8, 896, 2560], P('rep', 'dp'), parts along dimension 0
- output 4: bfloat16 [8, 2560, 896], P('rep', 'dp'), parts along dimension 0
There are 4 independent parts. A program takes and returns all parts, laid end to end along the dimension named above; an argument that names none is the same for every part.
All inputs are finite; a program needn't handle non-finite values.
Results may differ from a plain program's by a relative error of at most 0.018.
Values are sent between devices in bfloat16 or wider.
A program may use at most 768 MiB of HBM per device.

v0:
```python
import jax
import jax.numpy as jnp
from jax import lax

NAMES = ("w_gate", "w_up", "w_down")


def matmul(a, w):
    return jnp.dot(a, w, preferred_element_type=jnp.float32).astype(jnp.bfloat16)


def normed(h):
    wide = h.astype(jnp.float32)
    scale = lax.rsqrt(jnp.mean(wide**2, -1, keepdims=True) + 1e-6)
    return (wide * scale).astype(jnp.bfloat16)


def layer(h, w):
    a = normed(h)
    gate = jnp.dot(a, w["w_gate"], preferred_element_type=jnp.float32)
    up = jnp.dot(a, w["w_up"], preferred_element_type=jnp.float32)
    return h + matmul((jax.nn.silu(gate) * up).astype(jnp.bfloat16), w["w_down"])


def stack(weights, h):
    for number in range(weights["w_gate"].shape[0]):
        h = layer(h, {name: w[number] for name, w in weights.items()})
    return h


def solution(mesh):
    groups = mesh.shape["rep"]

    def step(x, dy, *weights):
        shape = x.shape
        x, dy = (t.reshape(groups, -1, *t.shape[1:]) for t in (x, dy))

        def of_a_group(x, dy):
            _, back = jax.vjp(stack, dict(zip(NAMES, weights, strict=True)), x)
            by_weights, by_x = back(dy)
            return (by_x, *(by_weights[name] for name in NAMES))

        by_x, *by_weights = jax.vmap(of_a_group)(x, dy)
        return (by_x.reshape(shape), *(t.reshape(-1, *t.shape[2:]) for t in by_weights))

    return step
```

profile of v0, /device:TPU:112, one launch (start us, length us, event | category | flops | bytes accessed | tf_op | source)
XLA Modules:
  0.0 1001.2 jit_solution(8672899709811470952)
XLA Ops:
  23.6 10.8 %copy.1 = bf16[1,4096,896]{1,2,0:T(8,128)(2,1)} copy(bf16[1,4096,896]{2,1,0:T(8,128)(2,1)} %param.1) | data formatting | bytes 14680064 | tf_op args[0]
  35.0 10.8 %copy = bf16[1,4096,896]{1,2,0:T(8,128)(2,1)} copy(bf16[1,4096,896]{2,1,0:T(8,128)(2,1)} %param) | data formatting | bytes 14680064 | tf_op args[1]
  45.8 15.0 %all-gather.30.cloned.1.call-done = bf16[1,896,2560]{2,1,0:T(8,128)(2,1)} async-done(((bf16[1,224,2560]{2,1,0:T(8,128)(2,1)}), bf16[1,896,2560]{2,1,0:T(8,128)(2,1)}) %all-gather.30.cloned.1.call-update) | async-done | bytes 4587536 | tf_op jit(solution)/vmap(jvp())/squeeze | solution.py:27
  60.8 29.3 %fusion.99 = f32[4096,2560]{1,0:T(8,128)} fusion(bf16[1,896,2560]{2,1,0:T(8,128)(2,1)} %all-gather.30.cloned.1.call-done, bf16[1,4096,896]{2,1,0:T(8,128)(2,1)} %param.1, f32[4096]{0:T(1024)S(1)} %get-tuple-element.13), kind=kOutput, calls=%fused_computation.101 | convolution fusion | flops 18801491968 | bytes 53886976 | tf_op jit(solution)/vmap(jvp())/dot_general | solution.py:20
  90.1 20.6 %all-gather.32.cloned.1.call-done = bf16[1,896,2560]{2,1,0:T(8,128)(2,1)} async-done(((bf16[1,224,2560]{2,1,0:T(8,128)(2,1)}), bf16[1,896,2560]{2,1,0:T(8,128)(2,1)}) %all-gather.32.cloned.1.call-update) | async-done | bytes 4587536 | tf_op jit(solution)/vmap(jvp())/squeeze | solution.py:27
  110.6 29.4 %fusion.95 = f32[4096,2560]{1,0:T(8,128)} fusion(bf16[1,896,2560]{2,1,0:T(8,128)(2,1)} %all-gather.32.cloned.1.call-done, bf16[1,4096,896]{2,1,0:T(8,128)(2,1)} %param.1, f32[4096]{0:T(1024)S(1)} %get-tuple-element.13), kind=kOutput, calls=%fused_computation.97 | convolution fusion | flops 18801491968 | bytes 53886976 | tf_op jit(solution)/vmap(jvp())/dot_general | solution.py:21
  140.0 34.3 %fusion.24 = bf16[4096,2560]{1,0:T(8,128)(2,1)} fusion(f32[4096,2560]{1,0:T(8,128)} %fusion.95, f32[4096,2560]{1,0:T(8,128)} %fusion.99), kind=kLoop, calls=%fused_computation.43 | loop fusion | flops 62914560 | bytes 104857600
  174.4 27.3 %fusion.40 = (f32[4096]{0:T(1024)S(1)}, bf16[1,1,4096,896]{2,3,1,0:T(8,128)(2,1)}) fusion(bf16[4096,2560]{1,0:T(8,128)(2,1)} %fusion.24, bf16[1,2560,896]{2,1,0:T(8,128)(2,1)} %all-gather.34.cloned.1.call-done, bf16[1,4096,896]{1,2,0:T(8,128)(2,1)} %copy.1), kind=kOutput, calls=%fused_computation.62 | convolution fusion | flops 18808827904 | bytes 40255488 | tf_op jit(solution)/vmap(jvp())/dot_general | solution.py:9
  209.7 29.5 %fusion.84 = f32[4096,2560]{1,0:T(8,128)} fusion(bf16[1,1,4096,896]{2,3,1,0:T(8,128)(2,1)} %get-tuple-element.15, f32[4096]{0:T(1024)S(1)} %bitcast.289, bf16[1,896,2560]{2,1,0:T(8,128)(2,1)} %all-gather.36.cloned.1.call-done), kind=kOutput, calls=%fused_computation.87 | convolution fusion | flops 18801491968 | bytes 53886976 | tf_op jit(solution)/vmap(jvp())/dot_general | solution.py:20
  239.2 20.2 %all-gather.40.cloned.1.call-done = bf16[1,896,2560]{2,1,0:T(8,128)(2,1)} async-done(((bf16[1,224,2560]{2,1,0:T(8,128)(2,1)}), bf16[1,896,2560]{2,1,0:T(8,128)(2,1)}) %all-gather.40.cloned.1.call-update) | async-done | bytes 4587536 | tf_op jit(solution)/vmap(jvp())/squeeze | solution.py:27
  259.4 29.6 %fusion.82 = f32[4096,2560]{1,0:T(8,128)} fusion(bf16[1,1,4096,896]{2,3,1,0:T(8,128)(2,1)} %get-tuple-element.15, f32[4096]{0:T(1024)S(1)} %bitcast.290, bf16[1,896,2560]{2,1,0:T(8,128)(2,1)} %all-gather.40.cloned.1.call-done), kind=kOutput, calls=%fused_computation.86 | convolution fusion | flops 18801491968 | bytes 53886976 | tf_op jit(solution)/vmap(jvp())/dot_general | solution.py:21
  289.0 19.6 %all-gather.38.cloned.1.call-done = bf16[1,2560,896]{2,1,0:T(8,128)(2,1)} async-done(((bf16[1,640,896]{2,1,0:T(8,128)(2,1)}), bf16[1,2560,896]{2,1,0:T(8,128)(2,1)}) %all-gather.38.cloned.1.call-update) | async-done | bytes 4587536 | tf_op jit(solution)/vmap(jvp())/squeeze | solution.py:27
  308.5 28.4 %convolution_convert_fusion.1 = bf16[4096,2560]{1,0:T(8,128)(2,1)} fusion(bf16[1,4096,896]{2,1,0:T(8,128)(2,1)} %param, bf16[1,2560,896]{2,1,0:T(8,128)(2,1)} %all-gather.38.cloned.1.call-done), kind=kOutput, calls=%fused_computation.39 | convolution fusion | flops 18800967680 | bytes 32899072 | tf_op jit(solution)/vmap(transpose(jvp()))/dot_general | solution.py:9
  336.9 33.6 %fusion.4 = bf16[4096,2560]{1,0:T(8,128)(2,1)S(1)} fusion(f32[4096,2560]{1,0:T(8,128)} %fusion.84, f32[4096,2560]{1,0:T(8,128)} %fusion.82, bf16[4096,2560]{1,0:T(8,128)(2,1)} %convolution_convert_fusion.1), kind=kLoop, calls=%fused_computation.10 | loop fusion | flops 125829120 | bytes 125829120
  377.7 27.2 %fusion.89 = bf16[4096,896]{0,1:T(8,128)(2,1)} fusion(bf16[4096,2560]{1,0:T(8,128)(2,1)S(1)} %fusion.4, bf16[1,896,2560]{2,1,0:T(8,128)(2,1)} %all-gather.36.cloned.1.call-done), kind=kOutput, calls=%fused_computation.91 | convolution fusion | flops 18790481920 | bytes 32899072 | tf_op jit(solution)/vmap(transpose(jvp()))/dot_general | solution.py:20
  404.9 38.1 %fusion.42 = (f32[4096]{0:T(1024)S(1)}, bf16[4096,896]{0,1:T(8,128)(2,1)}) fusion(bf16[1,1,4096,896]{2,3,1,0:T(8,128)(2,1)} %get-tuple-element.15, bf16[4096,896]{0,1:T(8,128)(2,1)} %fusion.89, bf16[1,896,2560]{2,1,0:T(8,128)(2,1)} %all-gather.40.cloned.1.call-done, bf16[4096,2560]{1,0:T(8,128)(2,1)} %convolution_convert_fusion.1, f32[4096,2560]{1,0:T(8,128)} %fusion.84), kind=kOutput, calls=%fused_computation.64 | convolution fusion | flops 18875412480 | bytes 89538560 | tf_op jit(solution)/vmap(transpose(jvp()))/dot_general | solution.py:21
  443.1 10.3 %fusion.47 = bf16[1,1,4096,896]{2,3,1,0:T(8,128)(2,1)S(1)} fusion(bf16[1,1,4096,896]{2,3,1,0:T(8,128)(2,1)} %get-tuple-element.15, bf16[4096,896]{0,1:T(8,128)(2,1)} %get-tuple-element.17, bf16[1,4096,896]{1,2,0:T(8,128)(2,1)} %copy, f32[4096]{0:T(1024)S(1)} %bitcast.288, f32[4096]{0:T(1024)S(1)} %bitcast.291), kind=kLoop, calls=%fused_computation.69 | loop fusion | flops 25690112 | bytes 29392896 | tf_op jit(solution)/vmap(transpose(jvp()))/add_any | solution.py:13
  456.2 26.8 %fusion.69 = f32[1,2560,896]{2,1,0:T(8,128)} fusion(bf16[4096,2560]{1,0:T(8,128)(2,1)} %fusion.24, bf16[1,1,4096,896]{2,3,1,0:T(8,128)(2,1)S(1)} %fusion.47), kind=kOutput, calls=%fused_computation.82 | convolution fusion | flops 18790481920 | bytes 37486592 | tf_op jit(solution)/vmap(transpose(jvp()))/dot_general | solution.py:9
  483.2 36.8 %fusion.72 = f32[1,2560,896]{2,1,0:T(8,128)} fusion(bf16[1,4096,896]{2,1,0:T(8,128)(2,1)} %param, f32[4096,2560]{1,0:T(8,128)} %fusion.82, f32[4096,2560]{1,0:T(8,128)} %fusion.84), kind=kOutput, calls=%fused_computation.84 | convolution fusion | flops 18853396480 | bytes 100401152 | tf_op jit(solution)/vmap(transpose(jvp()))/dot_general | solution.py:9
  520.1 27.9 %convolution_convert_fusion = bf16[4096,2560]{1,0:T(8,128)(2,1)} fusion(bf16[1,1,4096,896]{2,3,1,0:T(8,128)(2,1)} %copy-done, bf16[1,2560,896]{2,1,0:T(8,128)(2,1)} %all-gather.34.cloned.1.call-done), kind=kOutput, calls=%fused_computation.38 | convolution fusion | flops 18800967680 | bytes 32899072 | tf_op jit(solution)/vmap(transpose(jvp()))/dot_general | solution.py:9
  548.0 41.2 %fusion.7 = bf16[4096,2560]{1,0:T(8,128)(2,1)} fusion(f32[4096,2560]{1,0:T(8,128)} %fusion.99, f32[4096,2560]{1,0:T(8,128)} %fusion.95, bf16[4096,2560]{1,0:T(8,128)(2,1)} %convolution_convert_fusion), kind=kLoop, calls=%fused_computation.13 | loop fusion | flops 125829120 | bytes 125829120
  589.2 34.5 %fusion.77 = f32[1,896,2560]{2,1,0:T(8,128)} fusion(bf16[4096,2560]{1,0:T(8,128)(2,1)} %convolution_convert_fusion.1, f32[4096,2560]{1,0:T(8,128)} %fusion.84, bf16[1,1,4096,896]{2,3,1,0:T(8,128)(2,1)} %get-tuple-element.15, f32[4096]{0:T(1024)S(1)} %bitcast.292), kind=kOutput, calls=%fused_computation.85 | convolution fusion | flops 18864406528 | bytes 79446016 | tf_op jit(solution)/vmap(transpose(jvp()))/dot_general | solution.py:21
  623.8 25.1 %fusion.97 = bf16[4096,896]{0,1:T(8,128)(2,1)} fusion(bf16[4096,2560]{1,0:T(8,128)(2,1)} %fusion.7, bf16[1,896,2560]{2,1,0:T(8,128)(2,1)} %all-gather.30.cloned.1.call-done), kind=kOutput, calls=%fused_computation.99 | convolution fusion | flops 18790481920 | bytes 32899072 | tf_op jit(solution)/vmap(transpose(jvp()))/dot_general | solution.py:20
  649.0 38.2 %fusion.38 = (f32[4096]{0:T(1024)S(1)}, bf16[4096,896]{0,1:T(8,128)(2,1)}) fusion(bf16[1,4096,896]{1,2,0:T(8,128)(2,1)} %copy.1, bf16[4096,896]{0,1:T(8,128)(2,1)} %fusion.97, bf16[1,896,2560]{2,1,0:T(8,128)(2,1)} %all-gather.32.cloned.1.call-done, bf16[4096,2560]{1,0:T(8,128)(2,1)} %convolution_convert_fusion, f32[4096,2560]{1,0:T(8,128)} %fusion.99), kind=kOutput, calls=%fused_computation.60 | convolution fusion | flops 18875412480 | bytes 89538560 | tf_op jit(solution)/vmap(transpose(jvp()))/dot_general | solution.py:21
  687.8 34.9 %fusion.61 = f32[1,896,2560]{2,1,0:T(8,128)} fusion(bf16[4096,2560]{1,0:T(8,128)(2,1)} %convolution_convert_fusion, f32[4096,2560]{1,0:T(8,128)} %fusion.99, bf16[1,4096,896]{1,2,0:T(8,128)(2,1)} %copy.1, f32[4096]{0:T(1024)S(1)} %bitcast.294), kind=kOutput, calls=%fused_computation.80 | convolution fusion | flops 18864406528 | bytes 79446016 | tf_op jit(solution)/vmap(transpose(jvp()))/dot_general | solution.py:21
  722.9 25.6 %convolution_bitcast_fusion = f32[1,896,2560]{2,1,0:T(8,128)} fusion(bf16[4096,2560]{1,0:T(8,128)(2,1)} %copy-done.1, bf16[1,1,4096,896]{2,3,1,0:T(8,128)(2,1)} %get-tuple-element.15, f32[4096]{0:T(1024)S(1)} %bitcast.293), kind=kOutput, calls=%fused_computation.83 | convolution fusion | flops 18801491968 | bytes 37502976 | tf_op jit(solution)/vmap(transpose(jvp()))/dot_general | solution.py:20
  748.6 25.7 %fusion.66 = f32[1,896,2560]{2,1,0:T(8,128)} fusion(bf16[4096,2560]{1,0:T(8,128)(2,1)} %fusion.7, bf16[1,4096,896]{1,2,0:T(8,128)(2,1)} %copy.1, f32[4096]{0:T(1024)S(1)} %bitcast.295), kind=kOutput, calls=%fused_computation.81 | convolution fusion | flops 18801491968 | bytes 37502976 | tf_op jit(solution)/vmap(transpose(jvp()))/dot_general | solution.py:20
  774.4 12.4 %fusion.46 = bf16[1,4096,896]{1,2,0:T(8,128)(2,1)} fusion(bf16[1,1,4096,896]{2,3,1,0:T(8,128)(2,1)} %copy-done, bf16[4096,896]{0,1:T(8,128)(2,1)} %get-tuple-element.19, bf16[1,4096,896]{1,2,0:T(8,128)(2,1)} %copy.1, f32[4096]{0:T(1024)S(1)} %bitcast.297, f32[4096]{0:T(1024)S(1)} %bitcast.296), kind=kLoop, calls=%fused_computation.68 | loop fusion | flops 25690112 | bytes 29392896 | tf_op jit(solution)/reshape | solution.py:44
  786.7 10.8 %copy.2 = bf16[1,4096,896]{2,1,0:T(8,128)(2,1)} copy(bf16[1,4096,896]{1,2,0:T(8,128)(2,1)} %fusion.46) | data formatting | bytes 14680064
  804.5 16.7 %reduce-scatter.25.cloned.1.call-done = f32[1,224,2560]{2,1,0:T(8,128)} async-done(((f32[1,896,2560]{2,1,0:T(8,128)}), f32[1,224,2560]{2,1,0:T(8,128)}) %reduce-scatter.25.cloned.1.call-update) | async-done | bytes 2293776
  824.4 81.6 %reduce-scatter.19.cloned.1.call-done = f32[1,224,2560]{2,1,0:T(8,128)} async-done(((f32[1,896,2560]{2,1,0:T(8,128)}), f32[1,224,2560]{2,1,0:T(8,128)}) %reduce-scatter.19.cloned.1.call-update) | async-done | bytes 2293776
  907.9 83.0 %reduce-scatter.21.cloned.1.call-done = f32[1,224,2560]{2,1,0:T(8,128)} async-done(((f32[1,896,2560]{2,1,0:T(8,128)}), f32[1,224,2560]{2,1,0:T(8,128)}) %reduce-scatter.21.cloned.1.call-update) | async-done | bytes 2293776
  (67 shorter events, 51.5 us)
Async XLA Ops:
  7.2 53.6 %all-gather.30.cloned.1.call-start = ((), (), s32[]{:S(2)}) async-start(), calls=%async_computation.6 | async-start | bytes 5734400 | tf_op jit(solution)/vmap(jvp())/squeeze | solution.py:27
  10.5 100.2 %all-gather.32.cloned.1.call-start = ((), (), s32[]{:S(2)}) async-start(), calls=%async_computation.7 | async-start | bytes 5734400 | tf_op jit(solution)/vmap(jvp())/squeeze | solution.py:27
  13.7 160.6 %all-gather.34.cloned.1.call-start = ((), (), s32[]{:S(2)}) async-start(), calls=%async_computation.8 | async-start | bytes 5734400 | tf_op jit(solution)/vmap(jvp())/squeeze | solution.py:27
  17.1 192.6 %all-gather.36.cloned.1.call-start = ((), (), s32[]{:S(2)}) async-start(), calls=%async_computation.9 | async-start | bytes 5734400 | tf_op jit(solution)/vmap(jvp())/squeeze | solution.py:27
  17.7 241.7 %all-gather.40.cloned.1.call-start = ((), (), s32[]{:S(2)}) async-start(), calls=%async_computation.11 | async-start | bytes 5734400 | tf_op jit(solution)/vmap(jvp())/squeeze | solution.py:27
  18.4 290.2 %all-gather.38.cloned.1.call-start = ((), (), s32[]{:S(2)}) async-start(), calls=%async_computation.10 | async-start | bytes 5734400 | tf_op jit(solution)/vmap(jvp())/squeeze | solution.py:27
  19.0 778.6 %reduce-scatter.29.cloned.1.call-start = ((), (), s32[]{:S(2)}) async-start(), calls=%async_computation.17 | async-start | bytes 11468800
  201.7 0.6 copy-start.2
  202.3 57.1 %copy-start.4 = (f32[1,1,4096]{2,1,0:T(1,128)}, f32[1,1,4096]{2,1,0:T(1,128)S(1)}, u32[]{:S(2)}) copy-start(f32[1,1,4096]{2,1,0:T(1,128)S(1)} %rsqrt.23) | copy-start | bytes 49156
  370.6 7.1 copy-start.1
  404.9 38.1 %copy-start.3 = (f32[4096]{0:T(1024)S(1)}, f32[4096]{0:T(1024)}, u32[]{:S(2)}) copy-start(f32[4096]{0:T(1024)} %copy-done.2) | copy-start | bytes 49156
  404.9 38.2 %copy-start.5 = (f32[1,1,4096]{2,1,0:T(1,128)S(1)}, f32[1,1,4096]{2,1,0:T(1,128)}, u32[]{:S(2)}) copy-start(f32[1,1,4096]{2,1,0:T(1,128)} %copy-done.4) | copy-start | bytes 49156
  453.3 2.9 copy-start
  483.1 316.3 %reduce-scatter.27.cloned.1.call-start = ((), (), s32[]{:S(2)}) async-start(), calls=%async_computation.16 | async-start | bytes 11468800
  520.0 282.7 %reduce-scatter.23.cloned.1.call-start = ((), (), s32[]{:S(2)}) async-start(), calls=%async_computation.14 | async-start | bytes 11468800
  548.0 41.2 %copy-start.6 = (f32[1,1,4096]{2,1,0:T(1,128)S(1)}, f32[1,1,4096]{2,1,0:T(1,128)}, u32[]{:S(2)}) copy-start(f32[1,1,4096]{2,1,0:T(1,128)} %copy-done.4) | copy-start | bytes 49156
  623.8 197.4 %reduce-scatter.25.cloned.1.call-start = ((), (), s32[]{:S(2)}) async-start(), calls=%async_computation.15 | async-start | bytes 11468800
  649.0 38.2 %copy-start.9 = (f32[4096]{0:T(1024)S(1)}, f32[4096]{0:T(1024)}, u32[]{:S(2)}) copy-start(f32[4096]{0:T(1024)} %get-tuple-element.12) | copy-start | bytes 49156
  687.8 35.1 %copy-start.7 = (f32[1,1,4096]{2,1,0:T(1,128)S(1)}, f32[1,1,4096]{2,1,0:T(1,128)}, u32[]{:S(2)}) copy-start(f32[1,1,4096]{2,1,0:T(1,128)} %copy-done.4) | copy-start | bytes 49156
  722.8 183.3 %reduce-scatter.19.cloned.1.call-start = ((), (), s32[]{:S(2)}) async-start(), calls=%async_computation.12 | async-start | bytes 11468800
  748.5 25.8 %copy-start.8 = (f32[1,1,4096]{2,1,0:T(1,128)S(1)}, f32[1,1,4096]{2,1,0:T(1,128)}, u32[]{:S(2)}) copy-start(f32[1,1,4096]{2,1,0:T(1,128)} %get-tuple-element.11) | copy-start | bytes 49156
  748.6 242.3 %reduce-scatter.21.cloned.1.call-start = ((), (), s32[]{:S(2)}) async-start(), calls=%async_computation.13 | async-start | bytes 11468800
Sparse Core Ops, SparseCore 0:
  10.6 50.1 all-gather.29
  62.9 47.6 all-gather.31
  112.2 47.7 all-gather.33
  161.9 47.6 all-gather.35
  211.6 47.6 all-gather.39
  260.8 47.6 all-gather.37
  483.2 83.2 reduce-scatter.28
  568.9 82.5 reduce-scatter.26
  653.8 82.5 reduce-scatter.22
  738.6 82.5 reduce-scatter.24
  823.5 82.5 reduce-scatter.18
  908.3 82.5 reduce-scatter.20
where the time goes:
time: 1010 us; the launch traced here: 1000 us
  matrix products  514 us (51%)
  waiting for transfers between devices  266 us (26%)
  other arithmetic  153 us (15%)
  local copies, waits for them, and re-layouts  52.5 us (5%)
  between operations  14.6 us (1%)
    dot_general x6, matrix products, layer(): up = jnp.dot(a, w['w_up'], preferred_element_type=jnp.float32)  205 us
    unnamed x18, waiting for transfers between devices  184 us
    dot_general x6, matrix products, layer(): gate = jnp.dot(a, w['w_gate'], preferred_element_type=jnp.float32)  162 us
    dot_general x5, matrix products, matmul(): jnp.dot(a, w, preferred_element_type=jnp.float32).astype(jnp.bfloat16)  147 us
    unnamed x3, other arithmetic  109 us
    squeeze x6, waiting for transfers between devices, stack(): h = layer(h, {name: w[number] for name, w in weights.items()})  82.6 us
    unnamed x23, local copies, waits for them, and re-layouts  42.9 us
  transfers between devices with their start and end apart: 12, of which 8 were waited for; matrix products, arithmetic and copies ran while one was open for 54% of the time, Pallas kernels for 0%

commit v1 on v0

v1 whole, which is shorter than its diff:
```python
import functools

import jax
import jax.numpy as jnp
from jax import lax
from jax.experimental import pallas as pl
from jax.experimental.pallas import tpu as pltpu
from jax.sharding import PartitionSpec as P

F32, BF16 = jnp.float32, jnp.bfloat16
LANES = 128
VMEM_LIMIT = 62 * 1024 * 1024


def dot(a, b, dims=((1,), (0,))):
    return lax.dot_general(a, b, (dims, ((), ())), preferred_element_type=F32)


def rms_scale(wide):
    return lax.rsqrt(jnp.mean(wide * wide, -1, keepdims=True) + 1e-6)


def normed(h):
    wide = h.astype(F32)
    return (wide * rms_scale(wide)).astype(BF16)


def slot(d, rows, core, part):
    return pl.ds(pl.multiple_of(d * rows + core * part, 16), part)


class Item:
    def __init__(self, ref, own, columns=None):
        self.ref, self.own, self.columns = ref, own, columns

    def half(self, d, core, quarter=None):
        if self.columns is None:
            rows = self.ref.shape[0] // self.own
            part = rows // 2
            if quarter is None:
                return self.ref.at[slot(d, rows, core, part)]
            part //= 2
            return self.ref.at[slot(d, rows, 2 * core + quarter, part)]
        rows = self.ref.shape[1] // self.own
        first, width = self.columns
        if quarter is not None:
            width //= 2
            first += quarter * width
        return self.ref.at[:, slot(d, rows, core, rows // 2), pl.ds(first, width)]


def forward_kernel(dp, n, nt, x_ref, wg_in, wu_in, wd_in, h_ref, a_ref, g_ref, u_ref, wgu_out, wd_out, gu, wd0, kept_a, hidden, send_sem, recv_sem, own_sem, out_sem):
    p, i = pl.program_id(0), pl.program_id(1)
    step = p * nt + i
    tile, part = g_ref.shape[1:]
    rows = pl.ds(pl.multiple_of(i * tile, tile), tile)

    me, rep = lax.axis_index("dp"), lax.axis_index("rep")
    core = lax.rem(rep, 2)
    right, left, far = lax.rem(me + 1, dp), lax.rem(me + dp - 1, dp), lax.rem(me + 2, dp)
    to_right, to_left, to_partner = {"dp": right}, {"dp": left}, {"rep": rep + 1 - 2 * core}

    items = [Item(gu.at[0], dp, (j * part, part)) for j in range(n)]
    items += [Item(wd0, dp)]
    cut = 2 * part
    items += [Item(gu.at[1], dp, (0, cut)), Item(gu.at[1], dp, (cut, n * part - cut))]
    items += [Item(wd_out.at[1], dp)]
    last = len(items) - 1

    def copy(k, s, ref, device, src=None):
        return pltpu.make_async_remote_copy(
            src_ref=ref if src is None else src,
            dst_ref=ref,
            send_sem=send_sem.at[k, s],
            recv_sem=recv_sem.at[k, s],
            device_id=device,
            device_id_type=pl.DeviceIdType.MESH,
        )

    def near(k):
        t = items[k]
        half = t.half(me, core)
        src = None
        if k == last:
            size = half.shape[0]
            src = wd_in.at[1, pl.ds(pl.multiple_of(core * size, 16), size)]
        return [copy(k, 0, half, to_right, src), copy(k, 1, half, to_left, src)]

    def onward(k):
        t = items[k]
        return [
            copy(k, 2, t.half(left, core, 0), to_right),
            copy(k, 3, t.half(right, core, 1), to_left),
        ]

    def across(k, c):
        t = items[k]
        return [
            copy(k, 4, t.half(left, c), to_partner),
            copy(k, 5, t.half(right, c), to_partner),
            copy(k, 6, t.half(far, c, 0), to_partner),
            copy(k, 7, t.half(far, c, 1), to_partner),
        ]

    def send_near(k):
        for c in near(k):
            c.start()

    def send_on(k):
        t = items[k]
        copy(k, 0, t.half(left, core), to_right).wait_recv()
        copy(k, 1, t.half(right, core), to_left).wait_recv()
        for c in onward(k) + across(k, core)[:2]:
            c.start()

    def send_across(k):
        t = items[k]
        copy(k, 2, t.half(far, core, 0), to_right).wait_recv()
        copy(k, 3, t.half(far, core, 1), to_left).wait_recv()
        for c in across(k, core)[2:]:
            c.start()

    def arrive(k):
        for c in across(k, 1 - core):
            c.wait_recv()

    def own(k):
        wide = lambda layer, m, w: pltpu.make_async_copy(w.at[layer], gu.at[layer, m, slot(me, w.shape[1], 0, w.shape[1])], own_sem.at[k])
        down = wd_in.shape[1]
        return [
            lambda: wide(0, 0, wg_in),
            lambda: wide(0, 1, wu_in),
            lambda: pltpu.make_async_copy(wd_in.at[0], wd0.at[slot(me, down, 0, down)], own_sem.at[k]),
            lambda: wide(1, 0, wg_in),
            lambda: wide(1, 1, wu_in),
            lambda: pltpu.make_async_copy(wd_in.at[1], wd_out.at[1, slot(me, down, 0, down)], own_sem.at[k]),
        ][k]()

    def out(k):
        return pltpu.make_async_copy(*[(gu.at[0], wgu_out.at[0]), (wd0, wd_out.at[0]), (gu.at[1], wgu_out.at[1])][k], out_sem.at[k])

    @pl.when(step == 0)
    def _():
        barrier = pltpu.get_barrier_semaphore()
        for k in range(6):
            own(k).start()
        for device in (to_right, to_left, to_partner):
            pl.semaphore_signal(barrier, inc=1, device_id=device, device_id_type=pl.DeviceIdType.MESH)
        pl.semaphore_wait(barrier, 3)
        own(0).wait()
        own(1).wait()
        send_near(0)
        send_on(0)
        send_near(1)
        send_across(0)
        for k in range(2, 5):
            own(k).wait()
        arrive(0)

    def at(phase, tile_index, *actions):
        @pl.when(step == phase * nt + tile_index * nt // 8)
        def _():
            for f, k in actions:
                f(k)

    for k in range(1, n):
        s = 3 + 7 * (k - 1)
        at(0, s, (send_on, k), (send_near, k + 1))
        at(0, s + 3, (send_across, k))
        at(k, 0, (arrive, k))
    at(n - 1, 6, (send_on, n), (send_near, n + 1))
    at(n, 0, (send_across, n), (arrive, n), (lambda k: (out(0).start(), out(1).start()), 0))
    at(n, 4, (send_on, n + 1), (send_near, n + 2))
    at(n, 6, (send_across, n + 1))
    at(n + 1, 0, (arrive, n + 1))
    at(n + 2, 1, (send_on, n + 2), (send_near, n + 3))
    at(n + 2, 7, (send_across, n + 2))
    at(n + 3, 0, (arrive, n + 2), (lambda k: out(2).start(), 0))
    at(n + 4, 4, (send_on, n + 3))
    at(n + 5, 4, (send_across, n + 3))

    @pl.when(p == 0)
    def _():
        a = normed(x_ref[...])
        kept_a[rows] = a
        a_ref[0] = a

    def gate_up(layer, j):
        a = kept_a[rows]
        at = pl.ds(pl.multiple_of(j * part, part), part)
        g, u = dot(a, gu[layer, 0, :, at]), dot(a, gu[layer, 1, :, at])
        g_ref[0], u_ref[0] = g, u
        return g, u, at

    @pl.when(p < n)
    def _():
        g, u, at = gate_up(0, p)
        hidden[rows, at] = (g * jax.nn.sigmoid(g) * u).astype(BF16)

    @pl.when(p == n)
    def _():
        h = x_ref[...] + dot(hidden[rows, :], wd0[...]).astype(BF16)
        h_ref[...] = h
        a = normed(h)
        kept_a[rows] = a
        a_ref[0] = a

    @pl.when(p > n)
    def _():
        gate_up(1, p - n - 1)

    @pl.when(step == (2 * n + 1) * nt - 1)
    def _():
        arrive(last)
        for k in range(len(items)):
            for c in near(k) + onward(k) + across(k, core):
                c.wait_send()
        own(5).wait()
        for k in range(3):
            out(k).wait()


def forward(dp, n, x, wg, wu, wd, tile=512):
    tokens, d = x.shape
    ff = wg.shape[2]
    part, nt = ff // n, tokens // tile
    end = nt - 1

    def x_at(p, i):
        return jnp.where((p == 0) | (p == n), i, end), 0

    def h_at(p, i):
        return jnp.where(p < n, 0, jnp.where(p == n, i, end)), 0

    def a_at(p, i):
        return jnp.where(p < n, 0, 1), jnp.where((p == 0) | (p == n), i, end), 0

    def g_at(p, i):
        second = p > n
        return jnp.where(second, 1, 0), jnp.where(p == n, end, i), jnp.where(second, p - n - 1, jnp.minimum(p, n - 1))

    kept = pl.BlockSpec((1, tile, part), g_at)
    anywhere = pl.BlockSpec(memory_space=pl.ANY)
    wide = jax.ShapeDtypeStruct((2, tokens, ff), F32)
    return pl.pallas_call(
        functools.partial(forward_kernel, dp, n, nt),
        name="forward",
        grid=(2 * n + 1, nt),
        in_specs=[pl.BlockSpec((tile, d), x_at)] + [anywhere] * 3,
        out_specs=[pl.BlockSpec((tile, d), h_at), pl.BlockSpec((1, tile, d), a_at), kept, kept, anywhere, anywhere],
        out_shape=[
            jax.ShapeDtypeStruct((tokens, d), BF16),
            jax.ShapeDtypeStruct((2, tokens, d), BF16),
            wide,
            wide,
            jax.ShapeDtypeStruct((2, 2, d, ff), BF16),
            jax.ShapeDtypeStruct((2, ff, d), BF16),
        ],
        scratch_shapes=[
            pltpu.VMEM((2, 2, d, ff), BF16),
            pltpu.VMEM((ff, d), BF16),
            pltpu.VMEM((tokens, d), BF16),
            pltpu.VMEM((tokens, ff), BF16),
            pltpu.SemaphoreType.DMA((n + 4, 8)),
            pltpu.SemaphoreType.DMA((n + 4, 8)),
            pltpu.SemaphoreType.DMA((6,)),
            pltpu.SemaphoreType.DMA((3,)),
        ],
        compiler_params=pltpu.CompilerParams(
            dimension_semantics=("arbitrary", "arbitrary"), vmem_limit_bytes=67043328, collective_id=0, has_side_effects=True
        ),
        cost_estimate=pl.CostEstimate(flops=10 * tokens * d * ff, transcendentals=tokens * ff, bytes_accessed=16 * tokens * ff),
    )(x, wg, wu, wd)


def backward_kernel(dp, first, last, *refs):
    refs = list(refs)
    take = lambda k: [refs.pop(0) for _ in range(k)]
    a_ref, dy_ref = take(2)
    wg = jnp.concatenate([r[...] for r in take(dp)], axis=1)
    wu = jnp.concatenate([r[...] for r in take(dp)], axis=1)
    wd = jnp.concatenate([r[...] for r in take(dp)], axis=0)
    g = jnp.concatenate([r[...] for r in take(dp)], axis=1)
    u = jnp.concatenate([r[...] for r in take(dp)], axis=1)
    (da_in,) = (None,) if first else take(1)
    (h_ref,) = take(1) if last else (None,)
    da_ref, out_ref = take(2)
    acc_g, acc_u, acc_d = take(3)
    step, steps = pl.program_id(0), pl.num_programs(0)

    a, dy = a_ref[...], dy_ref[...]
    dh = dot(dy, wd, ((1,), (1,))).astype(BF16).astype(F32)
    s = jax.nn.sigmoid(g)
    silu = g * s
    hidden = (silu * u).astype(BF16)
    du = (dh * silu).astype(BF16)
    dg = (dh * u * (s * (1.0 + g * (1.0 - s)))).astype(BF16)
    da = dot(dg, wg, ((1,), (1,))) + dot(du, wu, ((1,), (1,)))
    if da_in is not None:
        da = da + da_in[...]
    if last:
        wide = h_ref[...].astype(F32)
        scale = rms_scale(wide)
        c = da.astype(BF16).astype(F32)
        back = scale * c - wide * (scale * scale * scale * jnp.mean(c * wide, -1, keepdims=True))
        da_ref[...] = dy + back.astype(BF16)
    else:
        da_ref[...] = da

    @pl.when(step == 0)
    def _():
        acc_g[...] = jnp.zeros_like(acc_g)
        acc_u[...] = jnp.zeros_like(acc_u)
        acc_d[...] = jnp.zeros_like(acc_d)

    acc_g[...] += dot(a, dg, ((0,), (0,)))
    acc_u[...] += dot(a, du, ((0,), (0,)))
    acc_d[...] += dot(dy, hidden, ((0,), (0,)))

    @pl.when(step == steps - 1)
    def _():
        d, part = acc_g.shape
        rows, run = d // dp, part // dp
        for owner in range(dp):
            for k, acc in enumerate((acc_g, acc_u)):
                for q in range(dp):
                    at = (k * dp + q) * rows
                    out_ref[owner, at : at + rows, :] = acc[owner * rows : (owner + 1) * rows, q * run : (q + 1) * run].astype(BF16)
            base = 2 * dp * rows
            for q in range(d // LANES):
                block = acc_d[q * LANES : (q + 1) * LANES, owner * run : (owner + 1) * run]
                out_ref[owner, base + q * run : base + (q + 1) * run, :] = block.T.astype(BF16)


def backward(dp, n, j, layer, a, dy, wgu, wd, g, u, da, h, tile=512):
    tokens, d = dy.shape
    ff = wd.shape[1]
    part = ff // n
    run = part // dp
    first, last = da is None, h is not None
    rows = pl.BlockSpec((tile, d), lambda i: (i, 0))
    of_layer = pl.BlockSpec((None, tile, d), lambda i: (layer, i, 0))
    one = pl.Buffered(1)
    columns = [pl.BlockSpec((None, None, d, run), lambda i, m=m, q=q: (layer, m, 0, q * n + j), pipeline_mode=one) for m in range(2) for q in range(dp)]
    lines = [pl.BlockSpec((None, run, d), lambda i, q=q: (layer, q * n + j, 0), pipeline_mode=one) for q in range(dp)]
    wide = [pl.BlockSpec((None, tile, run), lambda i, q=q: (layer, i, q * n + j)) for q in range(dp)]
    args = [a, dy] + [wgu] * 2 * dp + [wd] * dp + [g] * dp + [u] * dp
    specs = [of_layer, rows] + columns + lines + wide * 2
    if not first:
        args.append(da)
        specs.append(rows)
    if last:
        args.append(h)
        specs.append(rows)
    size = 3 * d
    return pl.pallas_call(
        functools.partial(backward_kernel, dp, first, last),
        name="backward",
        grid=(tokens // tile,),
        in_specs=specs,
        out_specs=[rows, pl.BlockSpec((dp, size, LANES), lambda i: (0, 0, 0), pipeline_mode=one)],
        out_shape=[jax.ShapeDtypeStruct((tokens, d), BF16 if last else F32), jax.ShapeDtypeStruct((dp, size, LANES), BF16)],
        scratch_shapes=[pltpu.VMEM((d, part), F32)] * 3,
        compiler_params=pltpu.CompilerParams(dimension_semantics=("arbitrary",), vmem_limit_bytes=VMEM_LIMIT),
        cost_estimate=pl.CostEstimate(
            flops=12 * tokens * d * part, transcendentals=tokens * part, bytes_accessed=8 * tokens * (part + 2 * d)
        ),
    )(*args)


def layer_back(dp, n, layer, a, dy, wgu, wd, g, u, h):
    da, sums = None, []
    for j in range(n):
        da, terms = backward(dp, n, j, layer, a, dy, wgu, wd, g, u, da, h if j == n - 1 else None)
        sums.append(lax.psum_scatter(terms, "dp", scatter_dimension=0, tiled=True)[0])
    return da, sums


def assemble_kernel(dp, n, layers, *refs):
    sums, outs = refs[: layers * n], refs[layers * n :]
    for layer in range(layers):
        for j in range(n):
            t = sums[layer * n + j]
            for m in range(2):
                rows = outs[m].shape[1]
                for q in range(dp):
                    at = (m * dp + q) * rows
                    outs[m][layer, :, (q * n + j) * LANES : (q * n + j + 1) * LANES] = t[at : at + rows, :]
            d = outs[2].shape[2]
            run = outs[2].shape[1] // n
            for q in range(d // LANES):
                at = 2 * d + q * run
                outs[2][layer, j * run : (j + 1) * run, q * LANES : (q + 1) * LANES] = t[at : at + run, :]


def assembled(dp, n, shapes, sums):
    layers = shapes[0][0]
    inside = pl.BlockSpec(memory_space=pltpu.VMEM)
    return pl.pallas_call(
        functools.partial(assemble_kernel, dp, n, layers),
        name="assemble",
        in_specs=[inside] * len(sums),
        out_specs=[inside] * 3,
        out_shape=[jax.ShapeDtypeStruct(s, BF16) for s in shapes],
        compiler_params=pltpu.CompilerParams(vmem_limit_bytes=VMEM_LIMIT),
    )(*sums)


def solution(mesh):
    dp = mesh.shape["dp"]

    def step(x, dy, wg, wu, wd):
        x, dy = x[0], dy[0]
        n = wg.shape[2] // (dp * LANES)
        h1, a, g, u, wgu, wdown = forward(dp, n, x, wg, wu, wd)
        dh1, sums1 = layer_back(dp, n, 1, a, dy, wgu, wdown, g, u, h1)
        dx, sums0 = layer_back(dp, n, 0, a, dh1, wgu, wdown, g, u, x)
        return (dx[None], *assembled(dp, n, [w.shape for w in (wg, wu, wd)], sums0 + sums1))

    tokens, w = P(("rep", "dp"), None, None), P(None, "dp", None)
    return jax.shard_map(
        step,
        mesh=mesh,
        in_specs=(tokens, tokens, w, w, w),
        out_specs=(tokens, *[P("rep", "dp", None)] * 3),
        check_vma=False,
    )
```

time: 1010 us -> 666 us (0.66)
  Pallas kernels: 0 us -> 577 us
  matrix products: 514 us -> 0 us
  waiting for transfers between devices: 266 us -> 65.3 us
  other arithmetic: 153 us -> 0 us
  local copies, waits for them, and re-layouts: 52.5 us -> 0 us
    pallas_call x0 -> x12, Pallas kernels: none -> 577 us  [the longest x10 377 us: backward(): pl.pallas_call(functools.partial(backward_kernel, dp, first, last), name=...]
    dot_general x17 -> x0, matrix products: 514 us -> none  [the longest x6 205 us: layer(): up = jnp.dot(a, w['w_up'], preferred_element_type=jnp.float32)]
    unnamed x18 -> x10, waiting for transfers between devices: 184 us -> 1.57 us
    unnamed x3 -> x0, other arithmetic: 109 us -> none
    squeeze x6 -> x0, waiting for transfers between devices: 82.6 us -> none  [stack(): h = layer(h, {name: w[number] for name, w in weights.items()})]
    reduce_scatter x0 -> x10, waiting for transfers between devices: none -> 63.7 us  [layer_back(): lax.psum_scatter(terms, 'dp', scatter_dimension=0, tiled=True)[0]]
    unnamed x23 -> x0, local copies, waits for them, and re-layouts: 42.9 us -> none
    reshape x4 -> x0, other arithmetic: 17 us -> none  [the longest x1 12.4 us: step(): by_x.reshape(shape)]
  transfers between devices with their start and end apart: 12 -> 10, of which waited for: 8 -> 2; matrix products, arithmetic and copies ran while one was open for 54% -> 0% of each run, Pallas kernels for 0% -> 52%
where the time goes in v1:
time: 666 us; the launch traced here: 659 us
  Pallas kernels  577 us (87%)
  waiting for transfers between devices  65.3 us (10%)
  between operations  14.7 us (2%)
    pallas_call x10, Pallas kernels, backward(): pl.pallas_call(functools.partial(backward_kernel, dp, first, last), name=...  377 us
    pallas_call x1, Pallas kernels, forward(): pl.pallas_call(functools.partial(forward_kernel, dp, n, nt), name='forwar...  194 us
    reduce_scatter x10, waiting for transfers between devices, layer_back(): lax.psum_scatter(terms, 'dp', scatter_dimension=0, tiled=True)[0]  63.7 us
  transfers between devices with their start and end apart: 10, of which 2 were waited for; matrix products, arithmetic and copies ran while one was open for 0% of the time, Pallas kernels for 52%

profile of v1, /device:TPU:112, one launch (start us, length us, event | category | flops | bytes accessed | tf_op | source)
XLA Modules:
  0.0 659.1 jit_solution(8327025438805748762)
XLA Ops:
  7.2 0.1 reduce-scatter.21.cloned.1.call-start
  7.2 193.5 %forward.1 = (bf16[4096,896]{1,0:T(8,128)(2,1)}, bf16[2,4096,896]{2,1,0:T(8,128)(2,1)}, f32[2,4096,2560]{2,1,0:T(8,128)}, f32[2,4096,2560]{2,1,0:T(8,128)}, bf16...) custom-call(bf16[4096,896]{1,0:T(8,128)(2,1)} %bitcast.18, bf16[2,224,2560]{2,1,0:T(8,128)(2,1)} %wg_in.1, ...), custom_call_target="tpu_custom_call" | custom-call | flops 93952409600 | bytes 167772160 | tf_op jit(solution)/shard_map/forward/pallas_call | solution.py:245
  200.8 35.9 %backward.10 = (f32[4096,896]{1,0:T(8,128)}, bf16[4,2688,128]{2,1,0:T(8,128)(2,1)}) custom-call(bf16[2,4096,896]{2,1,0:T(8,128)(2,1)} %get-tuple-element.33.refs_0_, bf16[4096,896]{1,0:T(8,128)(2,1)} %bitcast.13, bf16[2,2,896,2560]{3,2,1,0:T(8,128)(2,1)} %get-tuple-element.34.refs_2_.refs_3_.refs_4_.refs_5_.refs_6_.refs_7_.refs_8_.refs_9_, ...), custom_call_target="tpu_custom_call" | custom-call | flops 22548578304 | bytes 75497472 | tf_op jit(solution)/shard_map/backward/pallas_call | solution.py:356
  236.7 0.1 reduce-scatter.21.cloned.1.call-update
  236.7 0.5 reduce-scatter.23.cloned.1.call-start
  237.3 37.6 %backward.11 = (f32[4096,896]{1,0:T(8,128)}, bf16[4,2688,128]{2,1,0:T(8,128)(2,1)}) custom-call(bf16[2,4096,896]{2,1,0:T(8,128)(2,1)} %get-tuple-element.33.refs_0_, bf16[4096,896]{1,0:T(8,128)(2,1)} %bitcast.14, bf16[2,2,896,2560]{3,2,1,0:T(8,128)(2,1)} %get-tuple-element.34.refs_2_.refs_3_.refs_4_.refs_5_.refs_6_.refs_7_.refs_8_.refs_9_, ...), custom_call_target="tpu_custom_call" | custom-call | flops 22548578304 | bytes 75497472 | tf_op jit(solution)/shard_map/backward/pallas_call | solution.py:356
  274.9 0.1 reduce-scatter.23.cloned.1.call-update
  275.0 0.1 reduce-scatter.25.cloned.1.call-start
  275.1 37.4 %backward.12 = (f32[4096,896]{1,0:T(8,128)}, bf16[4,2688,128]{2,1,0:T(8,128)(2,1)}) custom-call(bf16[2,4096,896]{2,1,0:T(8,128)(2,1)} %get-tuple-element.33.refs_0_, bf16[4096,896]{1,0:T(8,128)(2,1)} %bitcast.15, bf16[2,2,896,2560]{3,2,1,0:T(8,128)(2,1)} %get-tuple-element.34.refs_2_.refs_3_.refs_4_.refs_5_.refs_6_.refs_7_.refs_8_.refs_9_, ...), custom_call_target="tpu_custom_call" | custom-call | flops 22548578304 | bytes 75497472 | tf_op jit(solution)/shard_map/backward/pallas_call | solution.py:356
  312.5 0.1 reduce-scatter.25.cloned.1.call-update
  312.6 0.2 reduce-scatter.29.cloned.1.call-start
  312.8 37.5 %backward.13 = (f32[4096,896]{1,0:T(8,128)}, bf16[4,2688,128]{2,1,0:T(8,128)(2,1)}) custom-call(bf16[2,4096,896]{2,1,0:T(8,128)(2,1)} %get-tuple-element.33.refs_0_, bf16[4096,896]{1,0:T(8,128)(2,1)} %bitcast.16, bf16[2,2,896,2560]{3,2,1,0:T(8,128)(2,1)} %get-tuple-element.34.refs_2_.refs_3_.refs_4_.refs_5_.refs_6_.refs_7_.refs_8_.refs_9_, ...), custom_call_target="tpu_custom_call" | custom-call | flops 22548578304 | bytes 75497472 | tf_op jit(solution)/shard_map/backward/pallas_call | solution.py:356
  350.3 39.6 %backward.14 = (bf16[4096,896]{1,0:T(8,128)(2,1)}, bf16[4,2688,128]{2,1,0:T(8,128)(2,1)}) custom-call(bf16[2,4096,896]{2,1,0:T(8,128)(2,1)} %get-tuple-element.33.refs_0_, bf16[4096,896]{1,0:T(8,128)(2,1)} %bitcast.17, bf16[2,2,896,2560]{3,2,1,0:T(8,128)(2,1)} %get-tuple-element.34.refs_2_.refs_3_.refs_4_.refs_5_.refs_6_.refs_7_.refs_8_.refs_9_, ...), custom_call_target="tpu_custom_call" | custom-call | flops 22548578304 | bytes 75497472 | tf_op jit(solution)/shard_map/backward/pallas_call | solution.py:356
  389.9 0.1 reduce-scatter.29.cloned.1.call-update
  390.0 0.1 reduce-scatter.27.cloned.1.call-start
  390.1 0.6 reduce-scatter.27.cloned.1.call-update
  390.6 0.3 reduce-scatter.11.cloned.1.call-start
  390.9 36.0 %backward.15 = (f32[4096,896]{1,0:T(8,128)}, bf16[4,2688,128]{2,1,0:T(8,128)(2,1)}) custom-call(bf16[2,4096,896]{2,1,0:T(8,128)(2,1)} %get-tuple-element.33.refs_0_, bf16[4096,896]{1,0:T(8,128)(2,1)} %get-tuple-element.43.refs_1_, bf16[2,2,896,2560]{3,2,1,0:T(8,128)(2,1)} %get-tuple-element.34.refs_2_.refs_3_.refs_4_.refs_5_.refs_6_.refs_7_.refs_8_.refs_9_, ...), custom_call_target="tpu_custom_call" | custom-call | flops 22548578304 | bytes 75497472 | tf_op jit(solution)/shard_map/backward/pallas_call | solution.py:356
  426.9 0.1 reduce-scatter.11.cloned.1.call-update
  427.0 0.1 reduce-scatter.13.cloned.1.call-start
  427.0 37.5 %backward.16 = (f32[4096,896]{1,0:T(8,128)}, bf16[4,2688,128]{2,1,0:T(8,128)(2,1)}) custom-call(bf16[2,4096,896]{2,1,0:T(8,128)(2,1)} %get-tuple-element.33.refs_0_, bf16[4096,896]{1,0:T(8,128)(2,1)} %get-tuple-element.43.refs_1_, bf16[2,2,896,2560]{3,2,1,0:T(8,128)(2,1)} %get-tuple-element.34.refs_2_.refs_3_.refs_4_.refs_5_.refs_6_.refs_7_.refs_8_.refs_9_, ...), custom_call_target="tpu_custom_call" | custom-call | flops 22548578304 | bytes 75497472 | tf_op jit(solution)/shard_map/backward/pallas_call | solution.py:356
  464.5 0.1 reduce-scatter.13.cloned.1.call-update
  464.6 0.1 reduce-scatter.15.cloned.1.call-start
  464.6 37.4 %backward.17 = (f32[4096,896]{1,0:T(8,128)}, bf16[4,2688,128]{2,1,0:T(8,128)(2,1)}) custom-call(bf16[2,4096,896]{2,1,0:T(8,128)(2,1)} %get-tuple-element.33.refs_0_, bf16[4096,896]{1,0:T(8,128)(2,1)} %get-tuple-element.43.refs_1_, bf16[2,2,896,2560]{3,2,1,0:T(8,128)(2,1)} %get-tuple-element.34.refs_2_.refs_3_.refs_4_.refs_5_.refs_6_.refs_7_.refs_8_.refs_9_, ...), custom_call_target="tpu_custom_call" | custom-call | flops 22548578304 | bytes 75497472 | tf_op jit(solution)/shard_map/backward/pallas_call | solution.py:356
  502.1 0.3 reduce-scatter.19.cloned.1.call-start
  502.4 37.6 %backward.18 = (f32[4096,896]{1,0:T(8,128)}, bf16[4,2688,128]{2,1,0:T(8,128)(2,1)}) custom-call(bf16[2,4096,896]{2,1,0:T(8,128)(2,1)} %get-tuple-element.33.refs_0_, bf16[4096,896]{1,0:T(8,128)(2,1)} %get-tuple-element.43.refs_1_, bf16[2,2,896,2560]{3,2,1,0:T(8,128)(2,1)} %get-tuple-element.34.refs_2_.refs_3_.refs_4_.refs_5_.refs_6_.refs_7_.refs_8_.refs_9_, ...), custom_call_target="tpu_custom_call" | custom-call | flops 22548578304 | bytes 75497472 | tf_op jit(solution)/shard_map/backward/pallas_call | solution.py:356
  540.1 40.2 %backward.19 = (bf16[4096,896]{1,0:T(8,128)(2,1)}, bf16[4,2688,128]{2,1,0:T(8,128)(2,1)}) custom-call(bf16[2,4096,896]{2,1,0:T(8,128)(2,1)} %get-tuple-element.33.refs_0_, bf16[4096,896]{1,0:T(8,128)(2,1)} %get-tuple-element.43.refs_1_, bf16[2,2,896,2560]{3,2,1,0:T(8,128)(2,1)} %get-tuple-element.34.refs_2_.refs_3_.refs_4_.refs_5_.refs_6_.refs_7_.refs_8_.refs_9_, ...), custom_call_target="tpu_custom_call" | custom-call | flops 22548578304 | bytes 75497472 | tf_op jit(solution)/shard_map/backward/pallas_call | solution.py:356
  580.4 0.1 reduce-scatter.17.cloned.1.call-start
  580.4 0.6 reduce-scatter.17.cloned.1.call-update
  581.2 30.7 %reduce-scatter.19.cloned.1.call-done = bf16[1,2688,128]{2,1,0:T(8,128)(2,1)} async-done(((bf16[4,2688,128]{2,1,0:T(8,128)(2,1)}), bf16[1,2688,128]{2,1,0:T(8,128)(2,1)}) %reduce-scatter.19.cloned.1.call-update) | async-done | bytes 688144 | tf_op jit(solution)/shard_map/reduce_scatter | solution.py:375
  611.9 32.9 %reduce-scatter.17.cloned.1.call-done = bf16[1,2688,128]{2,1,0:T(8,128)(2,1)} async-done(((bf16[4,2688,128]{2,1,0:T(8,128)(2,1)}), bf16[1,2688,128]{2,1,0:T(8,128)(2,1)}) %reduce-scatter.17.cloned.1.call-update) | async-done | bytes 688144 | tf_op jit(solution)/shard_map/reduce_scatter | solution.py:375
  644.8 7.0 %assemble.1 = (bf16[2,224,2560]{2,1,0:T(8,128)(2,1)}, bf16[2,224,2560]{2,1,0:T(8,128)(2,1)}, bf16[2,640,896]{2,1,0:T(8,128)(2,1)}) custom-call(bf16[2688,128]{1,0:T(8,128)(2,1)} %bitcast.25, bf16[2688,128]{1,0:T(8,128)(2,1)} %bitcast.26, bf16[2688,128]{1,0:T(8,128)(2,1)} %bitcast.27, bf16[2688,128]{1,0:T(8,128)(2,1)} %bitcast.29, ...), custom_call_target="tpu_custom_call" | custom-call | tf_op jit(solution)/shard_map/assemble/pallas_call | solution.py:399
  (10 shorter events, 0.3 us)
Async XLA Ops:
  7.2 573.8 %reduce-scatter.21.cloned.1.call-start = ((), (), s32[]{:S(2)}) async-start(), calls=%async_computation.15 | async-start | bytes 3440640 | tf_op jit(solution)/shard_map/reduce_scatter | solution.py:375
  236.7 344.3 %reduce-scatter.23.cloned.1.call-start = ((), (), s32[]{:S(2)}) async-start(), calls=%async_computation.16 | async-start | bytes 3440640 | tf_op jit(solution)/shard_map/reduce_scatter | solution.py:375
  275.0 306.1 %reduce-scatter.25.cloned.1.call-start = ((), (), s32[]{:S(2)}) async-start(), calls=%async_computation.17 | async-start | bytes 3440640 | tf_op jit(solution)/shard_map/reduce_scatter | solution.py:375
  312.6 268.5 %reduce-scatter.29.cloned.1.call-start = ((), (), s32[]{:S(2)}) async-start(), calls=%async_computation.19 | async-start | bytes 3440640 | tf_op jit(solution)/shard_map/reduce_scatter | solution.py:375
  390.0 191.1 %reduce-scatter.27.cloned.1.call-start = ((), (), s32[]{:S(2)}) async-start(), calls=%async_computation.18 | async-start | bytes 3440640 | tf_op jit(solution)/shard_map/reduce_scatter | solution.py:375
  390.6 190.5 %reduce-scatter.11.cloned.1.call-start = ((), (), s32[]{:S(2)}) async-start(), calls=%async_computation.10 | async-start | bytes 3440640 | tf_op jit(solution)/shard_map/reduce_scatter | solution.py:375
  427.0 154.2 %reduce-scatter.13.cloned.1.call-start = ((), (), s32[]{:S(2)}) async-start(), calls=%async_computation.11 | async-start | bytes 3440640 | tf_op jit(solution)/shard_map/reduce_scatter | solution.py:375
  464.6 116.6 %reduce-scatter.15.cloned.1.call-start = ((), (), s32[]{:S(2)}) async-start(), calls=%async_computation.12 | async-start | bytes 3440640 | tf_op jit(solution)/shard_map/reduce_scatter | solution.py:375
  502.1 109.8 %reduce-scatter.19.cloned.1.call-start = ((), (), s32[]{:S(2)}) async-start(), calls=%async_computation.14 | async-start | bytes 3440640 | tf_op jit(solution)/shard_map/reduce_scatter | solution.py:375
  580.4 64.4 %reduce-scatter.17.cloned.1.call-start = ((), (), s32[]{:S(2)}) async-start(), calls=%async_computation.13 | async-start | bytes 3440640 | tf_op jit(solution)/shard_map/reduce_scatter | solution.py:375
Sparse Core Ops, SparseCore 0:
  236.9 31.3 reduce-scatter.20
  275.1 31.3 reduce-scatter.22
  312.7 31.3 reduce-scatter.24
  390.1 31.3 reduce-scatter.28
  423.7 30.6 reduce-scatter.26
  456.6 30.6 reduce-scatter.10
  489.6 30.6 reduce-scatter.12
  522.6 30.6 reduce-scatter.14
  580.5 31.3 reduce-scatter.18
  614.0 30.6 reduce-scatter.16

commit v2 on v1

--- a/solution.py
+++ b/solution.py
@@ -163,21 +163,23 @@
             for f, k in actions:
                 f(k)
 
+    at(0, 3, (send_on, 1), (send_near, 2), (send_near, 3))
+    at(0, 6, (send_across, 1))
+    for k, step_on, step_across in ((2, 9, 14), (3, 13, 20), (4, 18, 30)):
+        at(0, step_on, (send_on, k), (send_near, k + 2))
+        at(0, step_across, (send_across, k))
     for k in range(1, n):
-        s = 3 + 7 * (k - 1)
-        at(0, s, (send_on, k), (send_near, k + 1))
-        at(0, s + 3, (send_across, k))
         at(k, 0, (arrive, k))
-    at(n - 1, 6, (send_on, n), (send_near, n + 1))
+    at(0, 29, (send_on, n), (send_near, n + 2))
+    at(0, 38, (send_on, n + 1), (send_near, n + 3))
     at(n, 0, (send_across, n), (arrive, n), (lambda k: (out(0).start(), out(1).start()), 0))
-    at(n, 4, (send_on, n + 1), (send_near, n + 2))
+    at(n, 5, (send_on, n + 2))
     at(n, 6, (send_across, n + 1))
     at(n + 1, 0, (arrive, n + 1))
-    at(n + 2, 1, (send_on, n + 2), (send_near, n + 3))
-    at(n + 2, 7, (send_across, n + 2))
+    at(n + 1, 2, (send_on, n + 3))
+    at(n + 2, 1, (send_across, n + 2))
+    at(n + 2, 6, (send_across, n + 3))
     at(n + 3, 0, (arrive, n + 2), (lambda k: out(2).start(), 0))
-    at(n + 4, 4, (send_on, n + 3))
-    at(n + 5, 4, (send_across, n + 3))
 
     @pl.when(p == 0)
     def _():
@@ -273,7 +275,7 @@
     )(x, wg, wu, wd)
 
 
-def backward_kernel(dp, first, last, *refs):
+def backward_kernel(dp, first, last, after, *refs):
     refs = list(refs)
     take = lambda k: [refs.pop(0) for _ in range(k)]
     a_ref, dy_ref = take(2)
@@ -284,18 +286,20 @@
     u = jnp.concatenate([r[...] for r in take(dp)], axis=1)
     (da_in,) = (None,) if first else take(1)
     (h_ref,) = take(1) if last else (None,)
+    take(1 if after else 0)
     da_ref, out_ref = take(2)
     acc_g, acc_u, acc_d = take(3)
     step, steps = pl.program_id(0), pl.num_programs(0)
 
     a, dy = a_ref[...], dy_ref[...]
-    dh = dot(dy, wd, ((1,), (1,))).astype(BF16).astype(F32)
     s = jax.nn.sigmoid(g)
     silu = g * s
     hidden = (silu * u).astype(BF16)
+    slope = u * (s * (1.0 + g * (1.0 - s)))
+    dh = dot(dy, wd, ((1,), (1,))).astype(BF16).astype(F32)
     du = (dh * silu).astype(BF16)
-    dg = (dh * u * (s * (1.0 + g * (1.0 - s)))).astype(BF16)
-    da = dot(dg, wg, ((1,), (1,))) + dot(du, wu, ((1,), (1,)))
+    dg = (dh * slope).astype(BF16)
+    da = dot(jnp.concatenate([dg, du], axis=1), jnp.concatenate([wg, wu], axis=1), ((1,), (1,)))
     if da_in is not None:
         da = da + da_in[...]
     if last:
@@ -332,7 +336,7 @@
                 out_ref[owner, base + q * run : base + (q + 1) * run, :] = block.T.astype(BF16)
 
 
-def backward(dp, n, j, layer, a, dy, wgu, wd, g, u, da, h, tile=512):
+def backward(dp, n, j, layer, a, dy, wgu, wd, g, u, da, h, done, tile=512):
     tokens, d = dy.shape
     ff = wd.shape[1]
     part = ff // n
@@ -352,9 +356,12 @@
     if last:
         args.append(h)
         specs.append(rows)
+    if done is not None:
+        args.append(done)
+        specs.append(pl.BlockSpec(memory_space=pl.ANY))
     size = 3 * d
     return pl.pallas_call(
-        functools.partial(backward_kernel, dp, first, last),
+        functools.partial(backward_kernel, dp, first, last, done is not None),
         name="backward",
         grid=(tokens // tile,),
         in_specs=specs,
@@ -368,42 +375,68 @@
     )(*args)
 
 
-def layer_back(dp, n, layer, a, dy, wgu, wd, g, u, h):
-    da, sums = None, []
+def norm_kernel(da_ref, h_ref, dy_ref, done_ref, dx_ref):
+    wide = h_ref[...].astype(F32)
+    scale = rms_scale(wide)
+    c = da_ref[...].astype(BF16).astype(F32)
+    back = scale * c - wide * (scale * scale * scale * jnp.mean(c * wide, -1, keepdims=True))
+    dx_ref[...] = dy_ref[...] + back.astype(BF16)
+
+
+def norm_back(da, h, dy, done, tile=512):
+    tokens, d = dy.shape
+    rows = pl.BlockSpec((tile, d), lambda i: (i, 0))
+    return pl.pallas_call(
+        norm_kernel,
+        name="norm_back",
+        grid=(tokens // tile,),
+        in_specs=[rows, rows, rows, pl.BlockSpec(memory_space=pl.ANY)],
+        out_specs=rows,
+        out_shape=jax.ShapeDtypeStruct((tokens, d), BF16),
+        compiler_params=pltpu.CompilerParams(dimension_semantics=("arbitrary",)),
+        cost_estimate=pl.CostEstimate(flops=20 * tokens * d, transcendentals=tokens, bytes_accessed=10 * tokens * d),
+    )(da, h, dy, done)
+
+
+def layer_back(dp, n, layer, a, dy, wgu, wd, g, u, h, apart, before):
+    da, sums = None, list(before)
     for j in range(n):
-        da, terms = backward(dp, n, j, layer, a, dy, wgu, wd, g, u, da, h if j == n - 1 else None)
+        done = sums[-2] if len(sums) > 1 else None
+        da, terms = backward(dp, n, j, layer, a, dy, wgu, wd, g, u, da, h if j == n - 1 and not apart else None, done)
         sums.append(lax.psum_scatter(terms, "dp", scatter_dimension=0, tiled=True)[0])
-    return da, sums
-
-
-def assemble_kernel(dp, n, layers, *refs):
-    sums, outs = refs[: layers * n], refs[layers * n :]
-    for layer in range(layers):
-        for j in range(n):
-            t = sums[layer * n + j]
-            for m in range(2):
-                rows = outs[m].shape[1]
-                for q in range(dp):
-                    at = (m * dp + q) * rows
-                    outs[m][layer, :, (q * n + j) * LANES : (q * n + j + 1) * LANES] = t[at : at + rows, :]
-            d = outs[2].shape[2]
-            run = outs[2].shape[1] // n
-            for q in range(d // LANES):
-                at = 2 * d + q * run
-                outs[2][layer, j * run : (j + 1) * run, q * LANES : (q + 1) * LANES] = t[at : at + run, :]
-
-
-def assembled(dp, n, shapes, sums):
-    layers = shapes[0][0]
+    if apart:
+        da = norm_back(da, h, dy, sums[-2])
+    return da, sums[-n:]
+
+
+def assemble_kernel(dp, n, *refs):
+    sums, outs = refs[:n], refs[-3:]
+    for j in range(n):
+        t = sums[j]
+        for m in range(2):
+            rows = outs[m].shape[0]
+            for q in range(dp):
+                at = (m * dp + q) * rows
+                outs[m][:, (q * n + j) * LANES : (q * n + j + 1) * LANES] = t[at : at + rows, :]
+        d = outs[2].shape[1]
+        run = outs[2].shape[0] // n
+        for q in range(d // LANES):
+            at = 2 * d + q * run
+            outs[2][j * run : (j + 1) * run, q * LANES : (q + 1) * LANES] = t[at : at + run, :]
+
+
+def assembled(dp, n, shapes, layer, sums, others):
     inside = pl.BlockSpec(memory_space=pltpu.VMEM)
     return pl.pallas_call(
-        functools.partial(assemble_kernel, dp, n, layers),
+        functools.partial(assemble_kernel, dp, n),
         name="assemble",
-        in_specs=[inside] * len(sums),
-        out_specs=[inside] * 3,
+        grid=(1,),
+        in_specs=[inside] * n + [pl.BlockSpec(memory_space=pl.ANY)] * len(others),
+        out_specs=[pl.BlockSpec((None, *s[1:]), lambda i: (layer, 0, 0)) for s in shapes],
         out_shape=[jax.ShapeDtypeStruct(s, BF16) for s in shapes],
+        input_output_aliases={n + k: k for k in range(len(others))},
         compiler_params=pltpu.CompilerParams(vmem_limit_bytes=VMEM_LIMIT),
-    )(*sums)
+    )(*sums, *others)
 
 
 def solution(mesh):
@@ -413,9 +446,11 @@
         x, dy = x[0], dy[0]
         n = wg.shape[2] // (dp * LANES)
         h1, a, g, u, wgu, wdown = forward(dp, n, x, wg, wu, wd)
-        dh1, sums1 = layer_back(dp, n, 1, a, dy, wgu, wdown, g, u, h1)
-        dx, sums0 = layer_back(dp, n, 0, a, dh1, wgu, wdown, g, u, x)
-        return (dx[None], *assembled(dp, n, [w.shape for w in (wg, wu, wd)], sums0 + sums1))
+        dh1, sums1 = layer_back(dp, n, 1, a, dy, wgu, wdown, g, u, h1, False, [])
+        dx, sums0 = layer_back(dp, n, 0, a, dh1, wgu, wdown, g, u, x, True, sums1)
+        shapes = [w.shape for w in (wg, wu, wd)]
+        grads = assembled(dp, n, shapes, 1, sums1, [])
+        return (dx[None], *assembled(dp, n, shapes, 0, sums0, grads))
 
     tokens, w = P(("rep", "dp"), None, None), P(None, "dp", None)
     return jax.shard_map(

time: 666 us -> 615 us (0.923)
  waiting for transfers between devices: 65.3 us -> 13.1 us
    reduce_scatter x10, waiting for transfers between devices: 63.7 us -> 12.5 us  [layer_back(): lax.psum_scatter(terms, 'dp', scatter_dimension=0, tiled=True)[0]]
    pallas_call x11 -> x13, Pallas kernels: 384 us -> 392 us  [the longest x10 368 us: backward(): pl.pallas_call(functools.partial(backward_kernel, dp, first, last, done i...]
  transfers between devices with their start and end apart: 10 -> 10, of which waited for: 2 -> 1; matrix products, arithmetic and copies ran while one was open for 0% -> 0% of each run, Pallas kernels for 52% -> 58%
where the time goes in v2:
time: 615 us; the launch traced here: 608 us
  Pallas kernels  579 us (94%)
  between operations  14.5 us (2%)
  waiting for transfers between devices  13.1 us (2%)
    pallas_call x10, Pallas kernels, backward(): pl.pallas_call(functools.partial(backward_kernel, dp, first, last, done i...  368 us
    pallas_call x1, Pallas kernels, forward(): pl.pallas_call(functools.partial(forward_kernel, dp, n, nt), name='forwar...  187 us
    pallas_call x1, Pallas kernels, norm_back(): pl.pallas_call(norm_kernel, name='norm_back', grid=(tokens // tile,), in_...  15.3 us
    reduce_scatter x10, waiting for transfers between devices, layer_back(): lax.psum_scatter(terms, 'dp', scatter_dimension=0, tiled=True)[0]  12.5 us
  transfers between devices with their start and end apart: 10, of which 1 were waited for; matrix products, arithmetic and copies ran while one was open for 0% of the time, Pallas kernels for 58%

profile of v2, /device:TPU:112, one launch (start us, length us, event | category | flops | bytes accessed | tf_op | source)
XLA Modules:
  0.0 607.8 jit_solution(14586212164818564611)
XLA Ops:
  7.2 0.1 reduce-scatter.11.cloned.1.call-start
  7.2 187.0 %forward.1 = (bf16[4096,896]{1,0:T(8,128)(2,1)}, bf16[2,4096,896]{2,1,0:T(8,128)(2,1)}, f32[2,4096,2560]{2,1,0:T(8,128)}, f32[2,4096,2560]{2,1,0:T(8,128)}, bf16...) custom-call(bf16[4096,896]{1,0:T(8,128)(2,1)} %bitcast.18, bf16[2,224,2560]{2,1,0:T(8,128)(2,1)} %wg_in.1, ...), custom_call_target="tpu_custom_call" | custom-call | flops 93952409600 | bytes 167772160 | tf_op jit(solution)/shard_map/forward/pallas_call | solution.py:247
  194.2 36.0 %backward.10 = (f32[4096,896]{1,0:T(8,128)}, bf16[4,2688,128]{2,1,0:T(8,128)(2,1)}) custom-call(bf16[2,4096,896]{2,1,0:T(8,128)(2,1)} %get-tuple-element.36.refs_0_, bf16[4096,896]{1,0:T(8,128)(2,1)} %bitcast.13, bf16[2,2,896,2560]{3,2,1,0:T(8,128)(2,1)} %get-tuple-element.37.refs_2_.refs_3_.refs_4_.refs_5_.refs_6_.refs_7_.refs_8_.refs_9_, ...), custom_call_target="tpu_custom_call" | custom-call | flops 22548578304 | bytes 75497472 | tf_op jit(solution)/shard_map/backward/pallas_call | solution.py:363
  230.2 0.1 reduce-scatter.11.cloned.1.call-update
  230.2 0.2 reduce-scatter.13.cloned.1.call-start
  230.5 36.5 %backward.11 = (f32[4096,896]{1,0:T(8,128)}, bf16[4,2688,128]{2,1,0:T(8,128)(2,1)}) custom-call(bf16[2,4096,896]{2,1,0:T(8,128)(2,1)} %get-tuple-element.36.refs_0_, bf16[4096,896]{1,0:T(8,128)(2,1)} %bitcast.14, bf16[2,2,896,2560]{3,2,1,0:T(8,128)(2,1)} %get-tuple-element.37.refs_2_.refs_3_.refs_4_.refs_5_.refs_6_.refs_7_.refs_8_.refs_9_, ...), custom_call_target="tpu_custom_call" | custom-call | flops 22548578304 | bytes 75497472 | tf_op jit(solution)/shard_map/backward/pallas_call | solution.py:363
  267.0 0.1 reduce-scatter.13.cloned.1.call-update
  267.1 0.1 reduce-scatter.15.cloned.1.call-start
  267.2 36.6 %backward.12 = (f32[4096,896]{1,0:T(8,128)}, bf16[4,2688,128]{2,1,0:T(8,128)(2,1)}) custom-call(bf16[2,4096,896]{2,1,0:T(8,128)(2,1)} %get-tuple-element.36.refs_0_, bf16[4096,896]{1,0:T(8,128)(2,1)} %bitcast.15, bf16[2,2,896,2560]{3,2,1,0:T(8,128)(2,1)} %get-tuple-element.37.refs_2_.refs_3_.refs_4_.refs_5_.refs_6_.refs_7_.refs_8_.refs_9_, ...), custom_call_target="tpu_custom_call" | custom-call | flops 22548578304 | bytes 75497472 | tf_op jit(solution)/shard_map/backward/pallas_call | solution.py:363
  303.8 0.1 reduce-scatter.15.cloned.1.call-update
  303.8 0.1 reduce-scatter.17.cloned.1.call-start
  303.9 36.5 %backward.13 = (f32[4096,896]{1,0:T(8,128)}, bf16[4,2688,128]{2,1,0:T(8,128)(2,1)}) custom-call(bf16[2,4096,896]{2,1,0:T(8,128)(2,1)} %get-tuple-element.36.refs_0_, bf16[4096,896]{1,0:T(8,128)(2,1)} %bitcast.16, bf16[2,2,896,2560]{3,2,1,0:T(8,128)(2,1)} %get-tuple-element.37.refs_2_.refs_3_.refs_4_.refs_5_.refs_6_.refs_7_.refs_8_.refs_9_, ...), custom_call_target="tpu_custom_call" | custom-call | flops 22548578304 | bytes 75497472 | tf_op jit(solution)/shard_map/backward/pallas_call | solution.py:363
  340.5 0.3 reduce-scatter.19.cloned.1.call-start
  340.8 39.6 %backward.14 = (bf16[4096,896]{1,0:T(8,128)(2,1)}, bf16[4,2688,128]{2,1,0:T(8,128)(2,1)}) custom-call(bf16[2,4096,896]{2,1,0:T(8,128)(2,1)} %get-tuple-element.36.refs_0_, bf16[4096,896]{1,0:T(8,128)(2,1)} %bitcast.17, bf16[2,2,896,2560]{3,2,1,0:T(8,128)(2,1)} %get-tuple-element.37.refs_2_.refs_3_.refs_4_.refs_5_.refs_6_.refs_7_.refs_8_.refs_9_, ...), custom_call_target="tpu_custom_call" | custom-call | flops 22548578304 | bytes 75497472 | tf_op jit(solution)/shard_map/backward/pallas_call | solution.py:363
  380.5 0.1 reduce-scatter.21.cloned.1.call-start
  380.6 36.1 %backward.15 = (f32[4096,896]{1,0:T(8,128)}, bf16[4,2688,128]{2,1,0:T(8,128)(2,1)}) custom-call(bf16[2,4096,896]{2,1,0:T(8,128)(2,1)} %get-tuple-element.36.refs_0_, bf16[4096,896]{1,0:T(8,128)(2,1)} %get-tuple-element.49.refs_1_.dy_ref, bf16[2,2,896,2560]{3,2,1,0:T(8,128)(2,1)} %get-tuple-element.37.refs_2_.refs_3_.refs_4_.refs_5_.refs_6_.refs_7_.refs_8_.refs_9_, ...), custom_call_target="tpu_custom_call" | custom-call | flops 22548578304 | bytes 75497472 | tf_op jit(solution)/shard_map/backward/pallas_call | solution.py:363
  416.7 0.1 reduce-scatter.21.cloned.1.call-update
  416.8 0.5 reduce-scatter.23.cloned.1.call-start
  417.3 36.6 %backward.16 = (f32[4096,896]{1,0:T(8,128)}, bf16[4,2688,128]{2,1,0:T(8,128)(2,1)}) custom-call(bf16[2,4096,896]{2,1,0:T(8,128)(2,1)} %get-tuple-element.36.refs_0_, bf16[4096,896]{1,0:T(8,128)(2,1)} %get-tuple-element.49.refs_1_.dy_ref, bf16[2,2,896,2560]{3,2,1,0:T(8,128)(2,1)} %get-tuple-element.37.refs_2_.refs_3_.refs_4_.refs_5_.refs_6_.refs_7_.refs_8_.refs_9_, ...), custom_call_target="tpu_custom_call" | custom-call | flops 22548578304 | bytes 75497472 | tf_op jit(solution)/shard_map/backward/pallas_call | solution.py:363
  453.9 0.1 reduce-scatter.23.cloned.1.call-update
  453.9 0.1 reduce-scatter.25.cloned.1.call-start
  454.0 36.5 %backward.17 = (f32[4096,896]{1,0:T(8,128)}, bf16[4,2688,128]{2,1,0:T(8,128)(2,1)}) custom-call(bf16[2,4096,896]{2,1,0:T(8,128)(2,1)} %get-tuple-element.36.refs_0_, bf16[4096,896]{1,0:T(8,128)(2,1)} %get-tuple-element.49.refs_1_.dy_ref, bf16[2,2,896,2560]{3,2,1,0:T(8,128)(2,1)} %get-tuple-element.37.refs_2_.refs_3_.refs_4_.refs_5_.refs_6_.refs_7_.refs_8_.refs_9_, ...), custom_call_target="tpu_custom_call" | custom-call | flops 22548578304 | bytes 75497472 | tf_op jit(solution)/shard_map/backward/pallas_call | solution.py:363
  490.6 0.1 reduce-scatter.27.cloned.1.call-start
  490.7 36.6 %backward.18 = (f32[4096,896]{1,0:T(8,128)}, bf16[4,2688,128]{2,1,0:T(8,128)(2,1)}) custom-call(bf16[2,4096,896]{2,1,0:T(8,128)(2,1)} %get-tuple-element.36.refs_0_, bf16[4096,896]{1,0:T(8,128)(2,1)} %get-tuple-element.49.refs_1_.dy_ref, bf16[2,2,896,2560]{3,2,1,0:T(8,128)(2,1)} %get-tuple-element.37.refs_2_.refs_3_.refs_4_.refs_5_.refs_6_.refs_7_.refs_8_.refs_9_, ...), custom_call_target="tpu_custom_call" | custom-call | flops 22548578304 | bytes 75497472 | tf_op jit(solution)/shard_map/backward/pallas_call | solution.py:363
  527.3 0.1 reduce-scatter.27.cloned.1.call-update
  527.4 0.2 reduce-scatter.29.cloned.1.call-start
  527.7 36.7 %backward.19 = (f32[4096,896]{1,0:T(8,128)}, bf16[4,2688,128]{2,1,0:T(8,128)(2,1)}) custom-call(bf16[2,4096,896]{2,1,0:T(8,128)(2,1)} %get-tuple-element.36.refs_0_, bf16[4096,896]{1,0:T(8,128)(2,1)} %get-tuple-element.49.refs_1_.dy_ref, bf16[2,2,896,2560]{3,2,1,0:T(8,128)(2,1)} %get-tuple-element.37.refs_2_.refs_3_.refs_4_.refs_5_.refs_6_.refs_7_.refs_8_.refs_9_, ...), custom_call_target="tpu_custom_call" | custom-call | flops 22548578304 | bytes 75497472 | tf_op jit(solution)/shard_map/backward/pallas_call | solution.py:363
  564.4 0.1 reduce-scatter.29.cloned.1.call-update
  564.5 4.3 assemble.2
  568.8 15.3 %norm_back.1 = bf16[4096,896]{1,0:T(8,128)(2,1)} custom-call(f32[4096,896]{1,0:T(8,128)} %get-tuple-element.59.da_ref, bf16[4096,896]{1,0:T(8,128)(2,1)} %bitcast.19, bf16[4096,896]{1,0:T(8,128)(2,1)} %get-tuple-element.49.refs_1_.dy_ref, bf16[2688,128]{1,0:T(8,128)(2,1)} %bitcast.37), custom_call_target="tpu_custom_call" | custom-call | flops 73400320 | bytes 36700160 | tf_op jit(solution)/shard_map/norm_back/pallas_call | solution.py:389
  584.1 12.4 %reduce-scatter.29.cloned.1.call-done = bf16[1,2688,128]{2,1,0:T(8,128)(2,1)} async-done(((bf16[4,2688,128]{2,1,0:T(8,128)(2,1)}), bf16[1,2688,128]{2,1,0:T(8,128)(2,1)}) %reduce-scatter.29.cloned.1.call-update) | async-done | bytes 688144 | tf_op jit(solution)/shard_map/reduce_scatter | solution.py:406
  596.4 4.3 assemble.3
  (12 shorter events, 0.3 us)
Async XLA Ops:
  7.2 260.0 %reduce-scatter.11.cloned.1.call-start = ((), (), s32[]{:S(2)}) async-start(), calls=%async_computation.10 | async-start | bytes 3440640 | tf_op jit(solution)/shard_map/reduce_scatter | solution.py:406
  230.2 73.7 %reduce-scatter.13.cloned.1.call-start = ((), (), s32[]{:S(2)}) async-start(), calls=%async_computation.11 | async-start | bytes 3440640 | tf_op jit(solution)/shard_map/reduce_scatter | solution.py:406
  267.1 73.7 %reduce-scatter.15.cloned.1.call-start = ((), (), s32[]{:S(2)}) async-start(), calls=%async_computation.12 | async-start | bytes 3440640 | tf_op jit(solution)/shard_map/reduce_scatter | solution.py:406
  303.8 76.8 %reduce-scatter.17.cloned.1.call-start = ((), (), s32[]{:S(2)}) async-start(), calls=%async_computation.13 | async-start | bytes 3440640 | tf_op jit(solution)/shard_map/reduce_scatter | solution.py:406
  340.5 76.8 %reduce-scatter.19.cloned.1.call-start = ((), (), s32[]{:S(2)}) async-start(), calls=%async_computation.14 | async-start | bytes 3440640 | tf_op jit(solution)/shard_map/reduce_scatter | solution.py:406
  380.5 73.5 %reduce-scatter.21.cloned.1.call-start = ((), (), s32[]{:S(2)}) async-start(), calls=%async_computation.15 | async-start | bytes 3440640 | tf_op jit(solution)/shard_map/reduce_scatter | solution.py:406
  416.8 73.9 %reduce-scatter.23.cloned.1.call-start = ((), (), s32[]{:S(2)}) async-start(), calls=%async_computation.16 | async-start | bytes 3440640 | tf_op jit(solution)/shard_map/reduce_scatter | solution.py:406
  453.9 73.7 %reduce-scatter.25.cloned.1.call-start = ((), (), s32[]{:S(2)}) async-start(), calls=%async_computation.17 | async-start | bytes 3440640 | tf_op jit(solution)/shard_map/reduce_scatter | solution.py:406
  490.6 78.2 %reduce-scatter.27.cloned.1.call-start = ((), (), s32[]{:S(2)}) async-start(), calls=%async_computation.18 | async-start | bytes 3440640 | tf_op jit(solution)/shard_map/reduce_scatter | solution.py:406
  527.4 69.0 %reduce-scatter.29.cloned.1.call-start = ((), (), s32[]{:S(2)}) async-start(), calls=%async_computation.19 | async-start | bytes 3440640 | tf_op jit(solution)/shard_map/reduce_scatter | solution.py:406
Sparse Core Ops, SparseCore 0:
  230.4 31.7 reduce-scatter.10
  267.2 31.7 reduce-scatter.12
  303.9 31.7 reduce-scatter.14
  340.6 31.7 reduce-scatter.16
  380.6 31.7 reduce-scatter.18
  416.9 31.7 reduce-scatter.20
  454.0 31.7 reduce-scatter.22
  490.7 31.7 reduce-scatter.24
  527.5 31.7 reduce-scatter.26
  564.6 31.7 reduce-scatter.28
